TPU v7x, 32 devices: a whole 2x2x4 slice. The times are simulated.
32 devices in a mesh: section: 2 (over core), seq: 16 (over z, y, x).
Axes of the slice: x: 2, y: 2, z: 4, core: 2. Of those that a mesh axis runs over, the one named last changes fastest.
Arguments:
- acts: bfloat16 [2, 4096, 2048], P('section', 'seq'), may hold values from -6 to 6
- in_proj: bfloat16 [2, 2048, 4640], P('section', 'seq'), may hold values from -0.125 to 0.125
- out_proj: bfloat16 [2, 2048, 2048], P('section'), may hold values from -0.125 to 0.125
- conv_weight: float32 [2, 4, 2304], P('section'), may hold values from -3 to 3
- conv_bias: float32 [2, 2304], P('section'), may hold values from -3 to 3
- dt_bias: float32 [2, 32], P('section'), may hold values from -4 to -1
- decay_rate: float32 [2, 32], P('section'), may hold values from 0.0001 to 0.5
- skip_gain: float32 [2, 32], P('section'), may hold values from -4 to 4
- level_bias: float32 [2, 256], P('section'), may hold values from -4 to 4
- norm_gain: float32 [2, 2048], P('section'), may hold values from 0.5 to 1.5
- gate_gain: float32 [2, 2048], P('section'), may hold values from 0.5 to 1.5
Outputs:
- handoff: bfloat16 [2, 4096, 2048], P('section', 'seq')
All inputs are finite; a program needn't handle non-finite values.
Results may differ from a plain program's by a relative error of at most 0.006.
Values may be sent and summed in bfloat16 or wider, within the bound.
A program may use at most 128 MiB of HBM per device.

v0:
```python
import functools

import jax
import jax.numpy as jnp
from jax import lax
from jax.experimental import pallas as pl
from jax.experimental.pallas import tpu as pltpu
from jax.sharding import PartitionSpec as P

EPS = 1e-05
MESH = pl.DeviceIdType.MESH
f32 = jnp.float32
bf16 = jnp.bfloat16


def remote(src, dst, send, recv, seq):
    return pltpu.make_async_remote_copy(
        src_ref=src,
        dst_ref=dst,
        send_sem=send,
        recv_sem=recv,
        device_id={"seq": seq},
        device_id_type=MESH,
    )


def greet(seq):
    pl.semaphore_signal(
        pltpu.get_barrier_semaphore(), inc=1, device_id={"seq": seq}, device_id_type=MESH
    )


def partner(inner, step, group):
    low = lax.rem(lax.rem(inner, 2) + step % 2, 2)
    high = lax.rem(inner // 2 + step // 2, max(group // 2, 1))
    return high * 2 + low


def gather_kernel(
    group, n, starts, u_ref, w_ref, tail_ref, p_ref, halo_ref,
    u_all, w_all, acc, u_send, u_recv, w_send, up_send, down_send, w_recv,
    bc_up, bc_down, bc_peer, bc_recv, own_sem, halo_sem
):
    me = lax.axis_index("seq")
    outer = me // group
    inner = lax.rem(me, group)
    outers = n // group
    base = outer * group
    length = u_ref.shape[0]
    rows = w_ref.shape[0]
    depth = group * rows
    wide, bc_from, z_from = starts
    lanes = tail_ref.shape[2]
    main = 2 * wide + lanes
    columns = w_all.shape[2]
    has_up = outer < outers - 1
    has_down = outer > 0
    barrier = pltpu.get_barrier_semaphore()
    for step in range(1, group):
        greet(base + partner(inner, step, group))

    @pl.when(has_up)
    def _():
        greet(me + group)

    @pl.when(has_down)
    def _():
        greet(me - group)

    pl.semaphore_wait(
        barrier, group - 1 + has_up.astype(jnp.int32) + has_down.astype(jnp.int32)
    )

    def slot_at(source, slot, lo, hi):
        return w_all.at[source, pl.ds(pl.multiple_of(slot * rows, rows), rows), lo:hi]

    def main_slot(source, slot):
        return slot_at(source, slot, 0, main)

    def bc_slot(source, slot):
        return slot_at(source, slot, main, columns)

    def parts_for(peer):
        at = pl.multiple_of(peer * wide, wide)
        return (
            (w_ref.at[:, pl.ds(at, wide)], 0, wide),
            (w_ref.at[:, pl.ds(pl.multiple_of(z_from + at, 128), wide)], wide, 2 * wide),
            (tail_ref.at[peer], 2 * wide, main),
        )

    bc_src = w_ref.at[:, bc_from : bc_from + columns - main]

    def up(source, slot):
        at = source * group + slot
        piece = main_slot(source, slot)
        return remote(piece, piece, up_send.at[at], w_recv.at[at], me + group)

    def down(source, slot):
        at = source * group + slot
        piece = main_slot(source, slot)
        return remote(piece, piece, down_send.at[at], w_recv.at[at], me - group)

    def along(source, step):
        piece = bc_slot(source, inner)
        here = bc_recv.at[source * group + inner]
        if step > 0:
            return remote(piece, piece, bc_up.at[source], here, me + group)
        return remote(piece, piece, bc_down.at[source], here, me - group)

    def across(source, step):
        piece = bc_slot(source, inner)
        peer = base + partner(inner, step, group)
        at = source * group
        return remote(piece, piece, bc_peer.at[at + step], bc_recv.at[at + inner], peer)

    def arrived(source, slot):
        piece = main_slot(source, slot)
        remote(piece, piece, w_send.at[0], w_recv.at[source * group + slot], me).wait_recv()

    def bc_arrived(source, slot):
        piece = bc_slot(source, slot)
        remote(piece, piece, w_send.at[0], bc_recv.at[source * group + slot], me).wait_recv()

    for src, lo, hi in parts_for(inner):
        pltpu.make_async_copy(src, slot_at(outer, inner, lo, hi), own_sem.at[0]).start()
    pltpu.make_async_copy(bc_src, bc_slot(outer, inner), own_sem.at[0]).start()
    own_u = pltpu.make_async_copy(u_ref, u_all.at[inner], own_sem.at[1])
    own_u.start()
    def give(step):
        peer = partner(inner, step, group)
        for src, lo, hi in parts_for(peer):
            remote(
                src, slot_at(outer, inner, lo, hi), w_send.at[step], w_recv.at[me], base + peer
            ).start()

    for step in range(1, min(group, 3)):
        give(step)
    whole_slot = slot_at(outer, inner, 0, columns)
    pltpu.make_async_copy(whole_slot, whole_slot, own_sem.at[0]).wait()

    @pl.when(has_up)
    def _():
        up(outer, inner).start()
        along(outer, 1).start()

    @pl.when(has_down)
    def _():
        down(outer, inner).start()
        along(outer, -1).start()

    for step in range(1, group):
        slot = partner(inner, step, group)
        arrived(outer, slot)
        if step == 1:
            for far in range(3, group):
                give(far)

        @pl.when(has_up)
        def _():
            up(outer, slot).start()

        @pl.when(has_down)
        def _():
            down(outer, slot).start()

    sends = []
    for step in range(1, group):
        peer = partner(inner, step, group)
        copy = remote(u_ref, u_all.at[inner], u_send.at[step], u_recv.at[inner], base + peer)
        copy.start()
        sends.append(copy)
        across(outer, step).start()

    chunked = depth % 128 == 0

    def multiply(source, block, first=False):
        if not chunked:
            return

        at = pl.multiple_of(source * depth, 128)
        part = jnp.dot(
            u_all[block, :, pl.ds(at, depth)], w_all[source], preferred_element_type=f32
        )
        if first:
            acc[block] = part
        else:
            acc[block] += part

    def ready(source):
        for step in range(1, group):
            bc_arrived(source, partner(inner, step, group))

    def multiply_both(distance, block):
        @pl.when(outer - distance >= 0)
        def _():
            @pl.when(block == 0)
            def _():
                ready(outer - distance)

            multiply(outer - distance, block)

        @pl.when(outer + distance < outers)
        def _():
            @pl.when(block == 0)
            def _():
                ready(outer + distance)

            multiply(outer + distance, block)

    def relay(distance, block):
        slot = partner(inner, block, group)

        @pl.when(outer - distance >= 0)
        def _():
            source = outer - distance
            arrived(source, slot)

            @pl.when(has_up)
            def _():
                up(source, slot).start()

            @pl.when(block == 0)
            def _():
                bc_arrived(source, inner)

                @pl.when(has_up)
                def _():
                    along(source, 1).start()

                for step in range(1, group):
                    across(source, step).start()

        @pl.when(outer + distance < outers)
        def _():
            source = outer + distance
            arrived(source, slot)

            @pl.when(has_down)
            def _():
                down(source, slot).start()

            @pl.when(block == 0)
            def _():
                bc_arrived(source, inner)

                @pl.when(has_down)
                def _():
                    along(source, -1).start()

                for step in range(1, group):
                    across(source, step).start()

    def relay_first(block, carry):
        relay(1, block)
        return carry

    def relay_second(block, carry):
        relay(2, block)
        return carry

    if outers > 1:
        lax.fori_loop(0, group, relay_first, 0)
    if outers > 2:
        lax.fori_loop(0, group, relay_second, 0)
    own_u.wait()
    for step in range(1, group):
        peer = partner(inner, step, group)
        remote(u_all.at[peer], u_all.at[peer], u_send.at[0], u_recv.at[peer], me).wait_recv()
    ready(outer)

    def own_work(block, carry):
        multiply(outer, block, True)
        if outers > 2:
            multiply_both(1, block)
        return carry

    lax.fori_loop(0, group, own_work, 0)

    def later(step, carry):
        distance = step // group
        block = lax.rem(step, group)
        relay(distance, block)
        multiply_both(distance - 1, block)
        return carry

    lax.fori_loop(3 * group, max(outers, 3) * group, later, 0)

    def finish(step, carry):
        if outers > 1:
            multiply_both(outers - 1, step)
        if chunked:
            p_ref[step] = acc[step].astype(p_ref.dtype)
        return carry

    lax.fori_loop(0, group, finish, 0)
    if not chunked:
        every = w_all[...].reshape(outers * depth, columns)

        def at_once(block, carry):
            part = jnp.dot(u_all[block], every, preferred_element_type=f32)
            p_ref[block] = part.astype(p_ref.dtype)
            return carry

        lax.fori_loop(0, group, at_once, 0)
    keep = halo_ref.shape[0]

    @pl.when(jnp.logical_not(has_down))
    def _():
        halo_ref[...] = jnp.zeros(halo_ref.shape, halo_ref.dtype)

    def drain(at, carry):
        source = at // group
        slot = lax.rem(at, group)

        @pl.when(jnp.logical_and(has_up, source <= outer))
        def _():
            up(source, slot).wait_send()

            @pl.when(slot == 0)
            def _():
                along(source, 1).wait_send()

        @pl.when(jnp.logical_and(has_down, source >= outer))
        def _():
            down(source, slot).wait_send()

            @pl.when(slot == 0)
            def _():
                along(source, -1).wait_send()

        @pl.when(slot == 0)
        def _():
            for step in range(1, group):
                across(source, step).wait_send()

        return carry

    lax.fori_loop(0, n, drain, 0)
    edge = remote(
        p_ref.at[group - 1, length - keep :], halo_ref, halo_sem.at[0], halo_sem.at[1], me + group
    )

    @pl.when(has_up)
    def _():
        edge.start()

    for copy in sends:
        copy.wait_send()
    for step in range(1, group):
        piece = main_slot(outer, inner)
        remote(piece, piece, w_send.at[step], w_recv.at[me], me).wait_send()

    @pl.when(has_up)
    def _():
        edge.wait_send()

    @pl.when(has_down)
    def _():
        edge.wait_recv()


def gathered(u, w, tails, n, starts):
    group, rows, lanes = tails.shape
    length = u.shape[0]
    outers = n // group
    wide, bc_from, z_from = starts
    columns = 2 * wide + lanes + z_from - bc_from
    dma = pltpu.SemaphoreType.DMA
    return pl.pallas_call(
        functools.partial(gather_kernel, group, n, starts),
        out_shape=(
            jax.ShapeDtypeStruct((group, length, columns), bf16),
            jax.ShapeDtypeStruct((16, columns), bf16),
        ),
        in_specs=[pl.BlockSpec(memory_space=pltpu.VMEM)] * 3,
        out_specs=[pl.BlockSpec(memory_space=pltpu.VMEM)] * 2,
        scratch_shapes=[
            pltpu.VMEM((group,) + u.shape, bf16),
            pltpu.VMEM((outers, group * rows, columns), bf16),
            pltpu.VMEM((group, length, columns), f32),
            dma((group,)),
            dma((group,)),
            dma((group,)),
            dma((n,)),
            dma((n,)),
            dma((n,)),
            dma((outers,)),
            dma((outers,)),
            dma((n,)),
            dma((n,)),
            dma((2,)),
            dma((2,)),
        ],
        compiler_params=pltpu.CompilerParams(
            collective_id=0, has_side_effects=True, vmem_limit_bytes=56 << 20
        ),
    )(u, w, tails)


def selector(lanes, wide, size, first, stride):
    row = lax.broadcasted_iota(jnp.int32, (lanes, wide), 0)
    head = lax.broadcasted_iota(jnp.int32, (lanes, wide), 1) // size
    return jnp.where(row == head * stride + first, 1.0, 0.0).astype(bf16)


def spread(value, pick):
    high = value.astype(bf16)
    low = (value - high.astype(f32)).astype(bf16)
    return jnp.dot(high, pick, preferred_element_type=f32) + jnp.dot(
        low, pick, preferred_element_type=f32
    )


def silu(value):
    return value / (1.0 + jnp.exp(-value))


def softplus(value):
    return jnp.maximum(value, 0.0) + jnp.log1p(jnp.exp(-jnp.abs(value)))


def state_kernel(
    dims, p_ref, before_ref, halo_ref, taps_ref, bias_ref, small_bias_ref, rate_ref, x_ref, bc_ref, small_ref, cum_ref, state_ref
):
    wide, state, size, taps = dims
    length = p_ref.shape[1]
    main = p_ref.shape[2] - 2 * state
    keep = halo_ref.shape[0]
    raw = jnp.concatenate([p_ref[0, :, :wide], p_ref[0, :, main:]], axis=1).astype(f32)
    last = jnp.where(
        pl.program_id(0) == 0, halo_ref[...].astype(f32), before_ref[0].astype(f32)
    )
    last = jnp.concatenate([last[:, :wide], last[:, main:]], axis=1)
    ext = jnp.concatenate([last, raw], axis=0)
    first = keep - taps + 1
    mixed = bias_ref[...] + taps_ref[taps - 1 :] * raw
    for k in range(taps - 1):
        mixed = mixed + taps_ref[k : k + 1] * ext[first + k : first + k + length]
    mixed = silu(mixed)
    x = mixed[:, :wide]
    x_ref[0] = x.astype(bf16)
    bc = mixed[:, wide:].astype(bf16)
    bc_ref[0] = bc
    small = softplus(p_ref[0, :, 2 * wide : main].astype(f32) + small_bias_ref[...])
    small_ref[0] = small
    rows = lax.broadcasted_iota(jnp.int32, (length, length), 0)
    cols = lax.broadcasted_iota(jnp.int32, (length, length), 1)
    below = jnp.where(cols <= rows, 1.0, 0.0)
    cum = jnp.dot(
        below,
        -small * rate_ref[...],
        precision=lax.Precision.HIGHEST,
        preferred_element_type=f32,
    )
    cum_ref[0] = cum
    tail = jnp.exp(cum[length - 1 :] - cum) * small
    faded = (x * spread(tail, selector(small.shape[1], wide, size, 0, 1))).astype(bf16)
    state_ref[0] = lax.dot_general(
        bc[:, :state], faded, (((0,), (0,)), ((), ())), preferred_element_type=f32
    )


def inside_kernel(dims, levels, x_ref, bc_ref, small_ref, cum_ref, skip_ref, y_ref):
    wide, state, size, _ = dims
    hs = wide // size
    length = x_ref.shape[1]
    lanes = small_ref.shape[2]
    bc = bc_ref[0]
    scores = lax.dot_general(
        bc[:, state:], bc[:, :state], (((1,), (1,)), ((), ())), preferred_element_type=f32
    )
    rows = lax.broadcasted_iota(jnp.int32, (length, length), 0)
    cols = lax.broadcasted_iota(jnp.int32, (length, length), 1)
    causal = cols <= rows
    small = small_ref[0]
    cum = cum_ref[0]
    cum_rows = jnp.transpose(cum)
    x = x_ref[0].astype(f32)
    stepped = (x * spread(small, selector(lanes, wide, size, 0, 1))).astype(bf16)
    parts = []
    for h in range(hs):
        differ = cum[:, h : h + 1] - cum_rows[h : h + 1, :]
        weights = jnp.exp(jnp.where(causal, differ, -1e30)) * scores
        parts.append(
            jnp.dot(
                weights.astype(bf16),
                stepped[:, h * size : (h + 1) * size],
                preferred_element_type=f32,
            )
        )
    y = jnp.concatenate(parts, axis=1)
    own = spread(small, selector(lanes, wide, size, hs, levels))
    y_ref[0] = y * own + skip_ref[...] * x


def outside_kernel(
    dims, levels, used, group, y_ref, bc_ref, bucket_ref, small_ref, cum_ref, p_ref, acts_ref, gain_ref, w_hbm,
    out_ref, q_own, q_got, w_ref, acc, w_sem, send_sem, recv_sem
):
    wide, state, size, _ = dims
    hs = wide // size
    lanes = small_ref.shape[2]
    me = lax.axis_index("seq")
    inner = lax.rem(me, group)
    base = me - inner
    load = pltpu.make_async_copy(w_hbm, w_ref, w_sem)
    load.start()
    for step in range(1, group):
        greet(base + partner(inner, group - step, group))
    pl.semaphore_wait(pltpu.get_barrier_semaphore(), group - 1)

    def copy_to(step):
        peer = partner(inner, group - step, group)
        return remote(
            q_own.at[peer], q_got.at[inner], send_sem.at[step], recv_sem.at[inner], base + peer
        )

    def work(step, carry):
        block = partner(inner, group - step, group)
        c = bc_ref[block, :, state:]
        small = small_ref[block]
        total = None
        for level in range(used):
            reads = jnp.dot(c, bucket_ref[block, level], preferred_element_type=f32)
            term = reads * spread(small, selector(lanes, wide, size, hs + level + 1, levels))
            total = term if total is None else total + term
        y = y_ref[block]
        if total is not None:
            y = y + total * spread(jnp.exp(cum_ref[block]), selector(lanes, wide, size, 0, 1))
        z = p_ref[block, :, wide : 2 * wide].astype(f32)
        q_own[block] = (y * silu(z)).astype(bf16)

        @pl.when(step > 1)
        def _():
            copy_to(step - 1).start()

        return carry

    lax.fori_loop(1, group + 1, work, 0)
    load.wait()

    def project(q, j):
        q = q.astype(f32)
        part = jnp.dot(
            (q * gain_ref[j]).astype(bf16), w_ref[j], preferred_element_type=f32
        )
        return part, jnp.sum(q * q, axis=1, keepdims=True)

    acc[...], squares = project(q_own[inner], inner)

    def add(step, squares):
        peer = partner(inner, group - step, group)
        remote(q_got.at[peer], q_got.at[peer], send_sem.at[0], recv_sem.at[peer], me).wait_recv()
        part, more = project(q_got[peer], peer)
        acc[...] += part
        return squares + more

    squares = lax.fori_loop(1, group, add, squares)
    scale = lax.rsqrt(squares / (wide * group) + EPS)
    out_ref[...] = (acts_ref[...].astype(f32) + acc[...] * scale).astype(bf16)
    for step in range(1, group):
        copy_to(step).wait_send()


def finished(dims, levels, used, args, acts, gains, w):
    group, wide, width = w.shape
    length = acts.shape[0]
    dma = pltpu.SemaphoreType.DMA
    vmem = pl.BlockSpec(memory_space=pltpu.VMEM)
    return pl.pallas_call(
        functools.partial(outside_kernel, dims, levels, used, group),
        out_shape=jax.ShapeDtypeStruct((length, width), bf16),
        in_specs=[vmem] * 8 + [pl.BlockSpec(memory_space=pl.ANY)],
        out_specs=vmem,
        scratch_shapes=[
            pltpu.VMEM((group, length, wide), bf16),
            pltpu.VMEM((group, length, wide), bf16),
            pltpu.VMEM(w.shape, bf16),
            pltpu.VMEM((length, width), f32),
            dma,
            dma((group,)),
            dma((group,)),
        ],
        compiler_params=pltpu.CompilerParams(
            collective_id=1, has_side_effects=True, vmem_limit_bytes=48 << 20
        ),
    )(*args, acts, gains, w)


def blocked(shape):
    rest = len(shape) - 1
    return pl.BlockSpec((1,) + tuple(shape[1:]), lambda b: (b,) + (0,) * rest)


def whole(shape):
    rest = len(shape)
    return pl.BlockSpec(tuple(shape), lambda b: (0,) * rest)


def per_block(kernel, group, split, fixed, outs, flops, edge=0):
    specs = [blocked(v.shape) for v in split]
    if edge:
        p = split[0]
        at = p.shape[1] // edge - 1
        specs.append(
            pl.BlockSpec((1, edge, p.shape[2]), lambda b: (jnp.maximum(b - 1, 0), at, 0))
        )
        split = split + (p,)
    order = split + fixed
    specs += [whole(v.shape) for v in fixed]
    moved = sum(v.size * v.dtype.itemsize for v in order)
    return pl.pallas_call(
        kernel,
        grid=(group,),
        out_shape=outs,
        in_specs=specs,
        out_specs=[blocked(o.shape) for o in outs],
        compiler_params=pltpu.CompilerParams(vmem_limit_bytes=40 << 20),
        cost_estimate=pl.CostEstimate(flops=flops, bytes_accessed=moved, transcendentals=0),
    )(*order)


def exchange_kernel(group, x_ref, out_ref, send_sem, recv_sem, own_sem):
    me = lax.axis_index("seq")
    inner = lax.rem(me, group)
    base = me - inner
    for step in range(1, group):
        greet(base + lax.rem(inner + step, group))
    pl.semaphore_wait(pltpu.get_barrier_semaphore(), group - 1)
    sends = []
    for step in range(1, group):
        peer = lax.rem(inner + step, group)
        copy = remote(
            x_ref.at[peer], out_ref.at[inner], send_sem.at[step], recv_sem.at[inner], base + peer
        )
        copy.start()
        sends.append(copy)
    own = pltpu.make_async_copy(x_ref.at[inner], out_ref.at[inner], own_sem)
    own.start()
    own.wait()
    for step in range(1, group):
        peer = lax.rem(inner + step, group)
        remote(x_ref.at[peer], out_ref.at[peer], send_sem.at[0], recv_sem.at[peer], me).wait_recv()
    for copy in sends:
        copy.wait_send()


def exchanged(x):
    group = x.shape[0]
    dma = pltpu.SemaphoreType.DMA
    return pl.pallas_call(
        functools.partial(exchange_kernel, group),
        out_shape=jax.ShapeDtypeStruct(x.shape, x.dtype),
        in_specs=[pl.BlockSpec(memory_space=pltpu.VMEM)],
        out_specs=pl.BlockSpec(memory_space=pltpu.VMEM),
        scratch_shapes=[dma((group,)), dma((group,)), dma],
        compiler_params=pltpu.CompilerParams(collective_id=1, has_side_effects=True),
    )(x)


def swapped(block, axis, apart):
    count = lax.axis_size(axis)
    route = []
    for low in range(count):
        high = low | 1 << apart
        if high != low and high < count:
            route += [(low, high), (high, low)]
    return lax.ppermute(block, axis, route)


def passed_along(value, axis, steps):
    count = lax.axis_size(axis)
    pairs = [(source, (source + steps) % count) for source in range(count)]
    return lax.ppermute(value, axis, pairs)


def per_device(
    acts,
    in_proj,
    out_proj,
    conv_weight,
    conv_bias,
    dt_bias,
    decay_rate,
    skip_gain,
    level_bias,
    norm_gain,
    gate_gain,
):
    n = lax.axis_size("seq")
    group = min(4, n)
    bits = group.bit_length() - 1
    position = lax.axis_index("seq")
    inner_at = lax.rem(position, group)
    hidden = acts[0].astype(f32)
    length = hidden.shape[0]
    inner = gate_gain.shape[1]
    heads = dt_bias.shape[1]
    head_size = inner // heads
    chans = conv_weight.shape[2]
    state = (chans - inner) // 2
    taps = conv_weight.shape[1]
    margin = taps - 1
    levels_all = level_bias.shape[1] // heads
    levels_used = n.bit_length() - 1
    wide = inner // group
    hs = heads // group
    tokens = group * length

    w = in_proj[0]
    rows = w.shape[0]
    tail = hs + hs * levels_all
    lanes = -(-tail // 128) * 128
    at = chans + inner
    tails = jnp.concatenate(
        [
            w[:, at : at + heads].reshape(rows, group, hs),
            w[:, at + heads :].reshape(rows, group, hs * levels_all),
        ],
        axis=2,
    )
    tails = jnp.swapaxes(jnp.pad(tails, ((0, 0), (0, 0), (0, lanes - tail))), 0, 1)
    u = (
        hidden * lax.rsqrt(jnp.mean(hidden * hidden, axis=1, keepdims=True) + EPS) * norm_gain[0]
    ).astype(bf16)
    p, halo = gathered(u, w, tails, n, (wide, inner, chans))

    def mine(vector, count):
        return lax.dynamic_slice_in_dim(vector, inner_at * count, count, axis=-1)

    dims = (wide, state, head_size, taps)
    taps_w = jnp.concatenate([mine(conv_weight[0][:, :inner], wide), conv_weight[0][:, inner:]], 1)
    taps_b = jnp.concatenate([mine(conv_bias[0][:inner], wide), conv_bias[0][inner:]], 0)[None]
    small_bias = jnp.concatenate([mine(dt_bias[0], hs), mine(level_bias[0], hs * levels_all)])
    small_bias = jnp.pad(small_bias, (0, lanes - tail))[None]
    rate = jnp.pad(mine(decay_rate[0], hs), (0, lanes - hs))[None]
    skip = jnp.repeat(mine(skip_gain[0], hs), head_size)[None]

    def shaped(kind, *sizes):
        return jax.ShapeDtypeStruct((group,) + sizes, kind)

    x, bc, small, cum, states = per_block(
        functools.partial(state_kernel, dims),
        group,
        (p,),
        (halo, taps_w, taps_b, small_bias, rate),
        (
            shaped(bf16, length, wide),
            shaped(bf16, length, 2 * state),
            shaped(f32, length, lanes),
            shaped(f32, length, lanes),
            shaped(f32, state, wide),
        ),
        2 * tokens * state * wide,
        16,
    )
    (y,) = per_block(
        functools.partial(inside_kernel, dims, levels_all),
        group,
        (x, bc, small, cum),
        (skip,),
        (shaped(f32, length, wide),),
        16 * tokens * length * wide,
    )
    ends = cum[:, length - 1, :hs]

    def faded(log, block):
        return jnp.exp(jnp.repeat(log, head_size))[None] * block

    buckets = [[] for _ in range(group)]
    summed = [states[b] for b in range(group)]
    logs = [ends[b] for b in range(group)]
    before = [jnp.zeros_like(ends[0]) for _ in range(group)]
    for bit in range(bits):
        half = 1 << bit
        merged, merged_logs = [], []
        for g in range(len(summed) // 2):
            low, high = summed[2 * g], summed[2 * g + 1]
            for b in range(2 * g * half, 2 * g * half + half):
                buckets[b].append(jnp.zeros_like(low))
            for b in range(2 * g * half + half, 2 * (g + 1) * half):
                buckets[b].append(faded(before[b], low))
                before[b] = before[b] + logs[2 * g]
            merged.append(faded(logs[2 * g + 1], low) + high)
            merged_logs.append(logs[2 * g] + logs[2 * g + 1])
        summed, logs = merged, merged_logs
    block_state, block_log = summed[0], logs[0]
    before_log = jnp.zeros_like(block_log)
    for bit in range(bits, levels_used):
        other_log, other_state = swapped((block_log, block_state.astype(bf16)), "seq", bit)
        other_state = other_state.astype(f32)
        upper = position >> bit & 1 == 1
        bucket = jnp.where(upper, faded(before_log, other_state), 0.0)
        for b in range(group):
            buckets[b].append(faded(before[b], bucket))
        merged_upper = faded(block_log, other_state) + block_state
        merged_lower = faded(other_log, block_state) + other_state
        block_state = jnp.where(upper, merged_upper, merged_lower)
        before_log = jnp.where(upper, before_log + other_log, before_log)
        block_log = block_log + other_log
    stacked = jnp.stack([jnp.stack(held) for held in buckets]).astype(bf16)
    result = finished(
        dims,
        levels_all,
        levels_used,
        (y, bc, stacked, small, cum, p),
        acts[0],
        gate_gain[0].reshape(group, 1, wide),
        out_proj[0].reshape(group, wide, -1),
    )
    moved = passed_along(result, "section", 1)
    return moved[None]


def solution(mesh):
    return jax.shard_map(
        per_device,
        mesh=mesh,
        in_specs=(
            P("section", "seq", None),
            P("section", "seq", None),
            P("section", None, None),
            P("section", None, None),
            P("section", None),
            P("section", None),
            P("section", None),
            P("section", None),
            P("section", None),
            P("section", None),
            P("section", None),
        ),
        out_specs=P("section", "seq", None),
        check_vma=False,
    )
```

profile of v0, /device:TPU:0, one launch (start us, length us, event | category | flops | bytes accessed | tf_op | source)
XLA Modules:
  0.0 159.7 jit_solution(2437222683368377727)
XLA Ops:
  0.0 0.8 slice.73
  0.8 0.8 slice.72
  1.6 1.7 %copy.13 = bf16[1,128,4640]{2,1,0:T(8,128)(2,1)S(1)} copy(bf16[1,128,4640]{1,2,0:T(8,128)(2,1)} %param.12) | data formatting | bytes 2375680 | tf_op args[1]
  4.6 1.3 fusion.2.u_ref
  5.9 0.8 fusion.23.tail_ref
  6.7 95.8 %shard_map.109 = (bf16[4,256,1408]{2,1,0:T(8,128)(2,1)}, bf16[16,1408]{1,0:T(8,128)(2,1)}) custom-call(bf16[256,2048]{1,0:T(8,128)(2,1)} %fusion.2.u_ref, bf16[128,4640]{1,0:T(8,128)(2,1)} %bitcast.106, bf16[4,128,128]{2,1,0:T(8,128)(2,1)} %fusion.23.tail_ref), custom_call_target="tpu_custom_call" | custom-call | tf_op jit(solution)/shard_map/pallas_call | solution.py:369
  102.5 1.8 %copy-done.1 = bf16[4,256,1408]{2,1,0:T(8,128)(2,1)S(1)} copy-done((bf16[4,256,1408]{2,1,0:T(8,128)(2,1)S(1)}, bf16[4,256,1408]{2,1,0:T(8,128)(2,1)}, u32[]{:S(2)}) %copy-start.1) | copy-done | bytes 2883608
  104.3 0.8 copy-done.12
  105.1 6.3 %shard_map.110 = (bf16[4,256,512]{2,1,0:T(8,128)(2,1)S(1)}, bf16[4,256,256]{2,1,0:T(8,128)(2,1)S(1)}, f32[4,256,128]{2,1,0:T(8,128)S(1)}, f32[4,256,128]{2,1,0:T(8,128)S(1)}, f32[4,128,512]{2,1,0:T(8,128)S(1)}) custom-call(bf16[4,256,1408]{2,1,0:T(8,128)(2,1)S(1)} %copy-done.1, bf16[4,256,1408]{2,1,0:T(8,128)(2,1)S(1)} %copy-done.1, ...), custom_call_target="tpu_custom_call" | custom-call | flops 134217728 | bytes 5828608 | tf_op jit(solution)/shard_map/pallas_call | solution.py:612
  111.4 0.8 copy-done.6
  112.2 0.8 copy-done.9
  113.0 1.0 copy-done.14
  114.0 2.4 %collective-permute-start.1 = (f32[8]{0:T(128)S(1)}, f32[8]{0:T(128)S(1)}, u32[]{:S(2)}, u32[]{:S(2)}) collective-permute-start(f32[8]{0:T(128)S(1)} %get-tuple-element.20), channel_id=1, source_target_pairs={{0,4},{4,0},{1,5},{5,1},{2,6},{6,2},{3,7},{7,3},{8,12},{12,8},{9,1... | collective-permute-start | bytes 104 | tf_op jit(solution)/shard_map/ppermute | solution.py:668
  116.4 0.8 copy-done.3
  117.8 0.7 fusion.41
  119.5 0.7 fusion.28
  120.8 0.6 fusion.29
  121.5 1.2 collective-permute-done
  122.8 0.9 fusion.27
  123.7 1.0 copy-done.4
  124.7 1.0 copy-done.7
  125.8 1.0 copy-done.10
  126.8 1.2 copy-done.15
  128.1 4.1 %shard_map.111.y_ref = f32[4,256,512]{2,1,0:T(8,128)S(1)} custom-call(bf16[4,256,512]{2,1,0:T(8,128)(2,1)S(1)} %copy-done.15, bf16[4,256,256]{2,1,0:T(8,128)(2,1)S(1)} %copy-done.7, f32[4,256,128]{2,1,0:T(8,128)S(1)} %copy-done.10, f32[4,256,128]{2,1,0:T(8,128)S(1)} %copy-done.4, f32[1,512]{1,0:T(1,128)S(1)} %broadcast_in_dim_reshape.3.skip_ref), custom_call_target="tpu_custom_call" | custom-call | flops 2147483648 | bytes 2623488 | tf_op jit(solution)/shard_map/pallas_call | solution.py:612
  132.3 0.7 exp.127
  132.9 1.1 fusion.18
  134.0 0.8 maximum_bitcast_fusion
  134.8 1.0 maximum_bitcast_fusion.3
  136.0 1.6 %pad_maximum_fusion.bucket_ref = bf16[4,4,128,512]{3,2,1,0:T(8,128)(2,1)} fusion(bf16[1,4,128,512]{3,2,1,0:T(8,128)(2,1)S(1)} %maximum_bitcast_fusion.3, bf16[1,4,128,512]{3,2,1,0:T(8,128)(2,1)S(1)} %get-tuple-element.44, bf16[1,4,128,512]{3,2,1,0:T(8,128)(2,1)S(1)} %get-tuple-element.43, bf16[1,4,128,512]{3,2,1,0:T(8,128)(2,1)S(1)} %maximum_bitcast_fusion), kind=kLoop, calls=%fused_computation.5 | loop fusion | flops 3145728 | bytes 4194304 | tf_op jit(solution)/shard_map/stack | solution.py:801
  137.7 18.3 %shard_map.112 = bf16[256,2048]{1,0:T(8,128)(2,1)S(1)} custom-call(f32[4,256,512]{2,1,0:T(8,128)S(1)} %shard_map.111.y_ref, bf16[4,256,256]{2,1,0:T(8,128)(2,1)S(1)} %copy-done.8, bf16[4,4,128,512]{3,2,1,0:T(8,128)(2,1)} %pad_maximum_fusion.bucket_ref, f32[4,256,128]{2,1,0:T(8,128)S(1)} %copy-done.11, f32[4,256,128]{2,1,0:T(8,128)S(1)} %copy-done.5, ...), custom_call_target="tpu_custom_call" | custom-call | tf_op jit(solution)/shard_map/pallas_call | solution.py:570
  156.1 2.6 %collective-permute-done.3 = bf16[256,2048]{1,0:T(8,128)(2,1)S(1)} collective-permute-done((bf16[256,2048]{1,0:T(8,128)(2,1)S(1)}, bf16[256,2048]{1,0:T(8,128)(2,1)S(1)}, u32[]{:S(2)}, u32[]{:S(2)}) %collective-permute-start.3) | collective-permute-done | bytes 1048608 | tf_op jit(solution)/shard_map/ppermute | solution.py:674
  158.7 1.0 copy.19
  (99 shorter events, 4.0 us)
Async XLA Ops:
  0.0 4.5 %copy-start = (f32[1,256]{1,0:T(1,128)S(1)}, f32[1,256]{1,0:T(1,128)}, u32[]{:S(2)}) copy-start(f32[1,256]{1,0:T(1,128)} %param.19) | copy-start | bytes 3076
  0.0 3.9 %slice-start.1 = ((f32[1,2304]{1,0:T(1,128)}), f32[1,2048]{1,0:T(1,128)S(1)}, s32[]{:S(2)}) async-start(f32[1,2304]{1,0:T(1,128)} %param.15), calls=%async_computation.1 | async-start | bytes 16384 | tf_op jit(solution)/shard_map/slice | solution.py:733
  0.0 3.9 %slice-start = ((f32[1,2304]{1,0:T(1,128)}), f32[1,256]{1,0:T(1,128)S(1)}, s32[]{:S(2)}) async-start(f32[1,2304]{1,0:T(1,128)} %param.15), calls=%async_computation | async-start | bytes 2048 | tf_op jit(solution)/shard_map/slice | solution.py:733
  0.0 3.4 %copy-start.25 = (f32[1,32]{1,0:T(1,128)S(1)}, f32[1,32]{1,0:T(1,128)}, u32[]{:S(2)}) copy-start(f32[1,32]{1,0:T(1,128)} %param.17) | copy-start | bytes 388
  0.0 3.4 %copy-start.24 = (f32[1,32]{1,0:T(1,128)S(1)}, f32[1,32]{1,0:T(1,128)}, u32[]{:S(2)}) copy-start(f32[1,32]{1,0:T(1,128)} %param.16) | copy-start | bytes 388
  0.0 3.5 %copy-start.2 = (bf16[1,256,2048]{2,1,0:T(8,128)(2,1)S(1)}, bf16[1,256,2048]{2,1,0:T(8,128)(2,1)}, u32[]{:S(2)}) copy-start(bf16[1,256,2048]{2,1,0:T(8,128)(2,1)} %param.11) | copy-start | bytes 3145732
  1.6 3.1 %copy-start.22 = (f32[1,2048]{1,0:T(1,128)S(1)}, f32[1,2048]{1,0:T(1,128)}, u32[]{:S(2)}) copy-start(f32[1,2048]{1,0:T(1,128)} %param.20) | copy-start | bytes 24580
  3.3 3.4 %copy-start.16 = (bf16[1,128,4640]{2,1,0:T(8,128)(2,1)}, bf16[1,128,4640]{2,1,0:T(8,128)(2,1)S(1)}, u32[]{:S(2)}) copy-start(bf16[1,128,4640]{2,1,0:T(8,128)(2,1)S(1)} %copy.13) | copy-start | bytes 3563524
  102.5 1.8 %copy-start.1 = (bf16[4,256,1408]{2,1,0:T(8,128)(2,1)S(1)}, bf16[4,256,1408]{2,1,0:T(8,128)(2,1)}, u32[]{:S(2)}) copy-start(bf16[4,256,1408]{2,1,0:T(8,128)(2,1)} %get-tuple-element.12.p_ref.before_ref) | copy-start | bytes 8650756
  105.1 13.5 %copy-start.26 = (f32[1,32]{1,0:T(1,128)S(1)}, f32[1,32]{1,0:T(1,128)}, u32[]{:S(2)}) copy-start(f32[1,32]{1,0:T(1,128)} %param.18) | copy-start | bytes 388
  111.4 0.8 copy-start.6
  112.2 0.8 copy-start.9
  113.0 1.0 copy-start.14
  114.0 6.8 %collective-permute-start.1 = (f32[8]{0:T(128)S(1)}, f32[8]{0:T(128)S(1)}, u32[]{:S(2)}, u32[]{:S(2)}) collective-permute-start(f32[8]{0:T(128)S(1)} %get-tuple-element.20), channel_id=1, source_target_pairs={{0,4},{4,0},{1,5},{5,1},{2,6},{6,2},{3,7},{7,3},{8,12},{12,8},{9,1... | collective-permute-start | bytes 104 | tf_op jit(solution)/shard_map/ppermute | solution.py:668
  116.4 0.8 copy-start.3
  117.8 5.0 %collective-permute-start = (bf16[128,512]{1,0:T(8,128)(2,1)S(1)}, bf16[128,512]{1,0:T(8,128)(2,1)S(1)}, u32[]{:S(2)}, u32[]{:S(2)}) collective-permute-start(bf16[128,512]{1,0:T(8,128)(2,1)S(1)} %get-tuple-element.21), channel_id=1, source_target_pairs={{0,4},{4,0},{1,5},{5,1},{2,6},{6,2},{3,7},{7,3},{8,12},{12,8},{9,1... | collective-permute-start | bytes 393224 | tf_op jit(solution)/shard_map/ppermute | solution.py:668
  119.5 4.2 %copy-start.21 = (f32[512]{0:T(512)}, f32[512]{0:T(512)S(1)}, u32[]{:S(2)}) copy-start(f32[512]{0:T(512)S(1)} %exp.140) | copy-start | bytes 6148
  123.7 9.2 %collective-permute-start.2 = (bf16[128,512]{1,0:T(8,128)(2,1)}, bf16[128,512]{1,0:T(8,128)(2,1)}, u32[]{:S(2)}, u32[]{:S(2)}) collective-permute-start(bf16[128,512]{1,0:T(8,128)(2,1)} %get-tuple-element.41), channel_id=1, source_target_pairs={{0,8},{8,0},{1,9},{9,1},{2,10},{10,2},{3,11},{11,3},{4,12},{12,4},... | collective-permute-start | bytes 393224 | tf_op jit(solution)/shard_map/ppermute | solution.py:668
  123.7 1.0 copy-start.4
  124.7 1.0 copy-start.7
  125.8 1.0 copy-start.10
  126.8 1.2 copy-start.15
  128.0 4.1 %copy-start.23 = (f32[8]{0:T(128)S(1)}, f32[8]{0:T(128)}, u32[]{:S(2)}) copy-start(f32[8]{0:T(128)} %get-tuple-element.45) | copy-start | bytes 100
  132.9 2.9 %copy-start.17 = (bf16[1,128,512]{2,1,0:T(8,128)(2,1)S(1)}, bf16[1,128,512]{2,1,0:T(8,128)(2,1)}, u32[]{:S(2)}) copy-start(bf16[1,128,512]{2,1,0:T(8,128)(2,1)} %get-tuple-element.25) | copy-start | bytes 393220
  132.9 2.9 %copy-start.18 = (bf16[1,128,512]{2,1,0:T(8,128)(2,1)S(1)}, bf16[1,128,512]{2,1,0:T(8,128)(2,1)}, u32[]{:S(2)}) copy-start(bf16[1,128,512]{2,1,0:T(8,128)(2,1)} %get-tuple-element.23) | copy-start | bytes 393220
  132.9 2.9 %copy-start.19 = (bf16[1,128,512]{2,1,0:T(8,128)(2,1)S(1)}, bf16[1,128,512]{2,1,0:T(8,128)(2,1)}, u32[]{:S(2)}) copy-start(bf16[1,128,512]{2,1,0:T(8,128)(2,1)} %get-tuple-element.39) | copy-start | bytes 393220
  132.9 2.9 %copy-start.20 = (bf16[1,128,512]{2,1,0:T(8,128)(2,1)S(1)}, bf16[1,128,512]{2,1,0:T(8,128)(2,1)}, u32[]{:S(2)}) copy-start(bf16[1,128,512]{2,1,0:T(8,128)(2,1)} %get-tuple-element.42) | copy-start | bytes 393220
  136.0 1.7 %copy-start.5 = (f32[4,256,128]{2,1,0:T(8,128)S(1)}, f32[4,256,128]{2,1,0:T(8,128)}, u32[]{:S(2)}) copy-start(f32[4,256,128]{2,1,0:T(8,128)} %copy-done.3) | copy-start | bytes 1572868
  136.0 1.7 %copy-start.8 = (bf16[4,256,256]{2,1,0:T(8,128)(2,1)S(1)}, bf16[4,256,256]{2,1,0:T(8,128)(2,1)}, u32[]{:S(2)}) copy-start(bf16[4,256,256]{2,1,0:T(8,128)(2,1)} %copy-done.6) | copy-start | bytes 1572868
  136.0 1.7 %copy-start.11 = (f32[4,256,128]{2,1,0:T(8,128)S(1)}, f32[4,256,128]{2,1,0:T(8,128)}, u32[]{:S(2)}) copy-start(f32[4,256,128]{2,1,0:T(8,128)} %copy-done.9) | copy-start | bytes 1572868
  136.0 1.7 %copy-start.13 = (f32[1,2048]{1,0:T(1,128)S(1)}, f32[1,2048]{1,0:T(1,128)}, u32[]{:S(2)}) copy-start(f32[1,2048]{1,0:T(1,128)} %param.21) | copy-start | bytes 24580
  156.0 2.7 %collective-permute-start.3 = (bf16[256,2048]{1,0:T(8,128)(2,1)S(1)}, bf16[256,2048]{1,0:T(8,128)(2,1)S(1)}, u32[]{:S(2)}, u32[]{:S(2)}) collective-permute-start(bf16[256,2048]{1,0:T(8,128)(2,1)S(1)} %shard_map.112), channel_id=1, source_target_pairs={{0,16},{16,0},{1,17},{17,1},{2,18},{18,2},{3,19},{19,3},{4,20},{20... | collective-permute-start | bytes 3145736 | tf_op jit(solution)/shard_map/ppermute | solution.py:674
  (1 other events, 0.8 us)
where the time goes:
time: 160 us
  Pallas kernels  124 us (78%)
  local copies, waits for them, and re-layouts  19.1 us (12%)
  other arithmetic  9.32 us (6%)
  waiting for transfers between devices  3.9 us (2%)
  starting transfers between devices  2.55 us (2%)
    pallas_call x1, Pallas kernels, gathered(): pl.pallas_call(functools.partial(gather_kernel, group, n, starts), out_sh...  95.8 us
    pallas_call x1, Pallas kernels, finished(): pl.pallas_call(functools.partial(outside_kernel, dims, levels, used, grou...  18.3 us
    unnamed x56, local copies, waits for them, and re-layouts  13.2 us
    pallas_call x2, Pallas kernels, per_block(): pl.pallas_call(kernel, grid=(group,), out_shape=outs, in_specs=specs, out...  10.4 us
    another operation x6, other arithmetic, per_device(): stacked = jnp.stack([jnp.stack(held) for held in buckets]).astype(bf16)  5.46 us
  transfers between devices with their start and end apart: 4, of which 2 were waited for; matrix products, arithmetic and copies ran while one was open for 3% of the time, Pallas kernels for 3%

commit v1 on v0

v1 whole, which is shorter than its diff:
```python
import functools

import jax
import jax.numpy as jnp
from jax import lax
from jax.experimental import pallas as pl
from jax.experimental.pallas import tpu as pltpu
from jax.sharding import PartitionSpec as P

EPS = 1e-05
MESH = pl.DeviceIdType.MESH
f32 = jnp.float32
bf16 = jnp.bfloat16
HIGHEST = lax.Precision.HIGHEST


def remote(src, dst, send, recv, seq, axis="seq"):
    return pltpu.make_async_remote_copy(
        src_ref=src,
        dst_ref=dst,
        send_sem=send,
        recv_sem=recv,
        device_id={axis: seq},
        device_id_type=MESH,
    )


def greet(seq, axis="seq"):
    pl.semaphore_signal(
        pltpu.get_barrier_semaphore(), inc=1, device_id={axis: seq}, device_id_type=MESH
    )


def partner(inner, step, group):
    low = lax.rem(lax.rem(inner, 2) + step % 2, 2)
    high = lax.rem(inner // 2 + step // 2, max(group // 2, 1))
    return high * 2 + low


def selector(lanes, wide, size, first, stride):
    row = lax.broadcasted_iota(jnp.int32, (lanes, wide), 0)
    head = lax.broadcasted_iota(jnp.int32, (lanes, wide), 1) // size
    return jnp.where(row == head * stride + first, 1.0, 0.0).astype(bf16)


def spread(value, pick):
    high = value.astype(bf16)
    low = (value - high.astype(f32)).astype(bf16)
    return jnp.dot(high, pick, preferred_element_type=f32) + jnp.dot(
        low, pick, preferred_element_type=f32
    )


def silu(value):
    return value / (1.0 + jnp.exp(-value))


def softplus(value):
    return jnp.maximum(value, 0.0) + jnp.log1p(jnp.exp(-jnp.abs(value)))


def layer_kernel(
    dims, group, n, levels, used, sections,
    acts_ref, w_hbm, wo_hbm, taps_ref, cbias_ref, small_bias_ref, rate_ref, skip_ref,
    norm_ref, gate_ref, out_ref,
    u_all, w_own, tail_v, w_a, w_z, w_o, p_a, halo, before_s, picks, x_s, bc_s, small_s, cum_s,
    st, bucket, whole_st, xs_own, xs_got, xl_own, xl_got, y_s, q_own, q_got, o_acc, o_v,
    load_sem, u_send, u_recv, w_send, up_send, down_send, w_recv,
    bc_up, bc_down, bc_peer, bc_recv, zg_send, zg_recv, zu_send, zd_send, z_recv,
    halo_sem, xs_sem, xl_sem, q_send, q_recv, ho_send, ho_recv,
):
    wide, state, size, taps, z_from, lanes = dims
    section = lax.axis_index("section")
    me = lax.axis_index("seq")
    outer = me // group
    inner = lax.rem(me, group)
    outers = n // group
    base = outer * group
    length = acts_ref.shape[0]
    rows = w_hbm.shape[0]
    depth = group * rows
    chunks, _, _, cw = w_z.shape
    hs = wide // size
    main = wide + lanes
    columns = main + 2 * state
    bc_from = group * wide
    bits = group.bit_length() - 1
    keep = halo.shape[0]
    has_up = outer < outers - 1
    has_down = outer > 0
    p1 = partner(inner, 1, group)
    p2 = partner(inner, 2, group)
    p3 = partner(inner, 3, group)

    def at_rows(slot):
        return pl.ds(pl.multiple_of(slot * rows, rows), rows)

    def slot_at(source, slot, lo, hi):
        return w_a.at[source, at_rows(slot), lo:hi]

    def main_slot(source, slot):
        return slot_at(source, slot, 0, main)

    def bc_slot(source, slot):
        return slot_at(source, slot, main, columns)

    def x_cols(peer):
        return pl.ds(pl.multiple_of(peer * wide, wide), wide)

    def z_cols(peer, c):
        return pl.ds(pl.multiple_of(z_from + peer * wide + c * cw, 128), cw)

    load_all = pltpu.make_async_copy(w_hbm, w_own, load_sem.at[0])
    load_all.start()
    load_x = pltpu.make_async_copy(
        w_hbm.at[:, x_cols(inner)], slot_at(outer, inner, 0, wide), load_sem.at[1]
    )
    load_x.start()
    load_bc = pltpu.make_async_copy(
        w_hbm.at[:, bc_from : bc_from + 2 * state], bc_slot(outer, inner), load_sem.at[2]
    )
    load_bc.start()

    count = group - 1 + has_up.astype(jnp.int32) + has_down.astype(jnp.int32) + 1
    for step in range(1, group):
        greet(base + partner(inner, step, group))

    @pl.when(has_up)
    def _():
        greet(me + group)

    @pl.when(has_down)
    def _():
        greet(me - group)

    def twin(bit):
        half = 1 << bit
        return me + half - 2 * half * lax.rem(me // half, 2)

    for bit in range(bits, used):
        greet(twin(bit))
    greet(lax.rem(section + sections - 1, sections), "section")
    pl.semaphore_wait(pltpu.get_barrier_semaphore(), count + used - bits)

    def up(source, slot):
        at = source * group + slot
        piece = main_slot(source, slot)
        return remote(piece, piece, up_send.at[at], w_recv.at[at], me + group)

    def down(source, slot):
        at = source * group + slot
        piece = main_slot(source, slot)
        return remote(piece, piece, down_send.at[at], w_recv.at[at], me - group)

    def along(source, step):
        piece = bc_slot(source, inner)
        here = bc_recv.at[source * group + inner]
        if step > 0:
            return remote(piece, piece, bc_up.at[source], here, me + group)
        return remote(piece, piece, bc_down.at[source], here, me - group)

    def across(source, step):
        piece = bc_slot(source, inner)
        peer = base + partner(inner, step, group)
        at = source * group
        return remote(piece, piece, bc_peer.at[at + step], bc_recv.at[at + inner], peer)

    def arrived(source, slot):
        piece = main_slot(source, slot)
        remote(piece, piece, w_send.at[0], w_recv.at[source * group + slot], me).wait_recv()

    def bc_arrived(source, slot):
        piece = bc_slot(source, slot)
        remote(piece, piece, w_send.at[0], bc_recv.at[source * group + slot], me).wait_recv()

    def give_x(step):
        peer = partner(inner, step, group)
        remote(
            w_own.at[:, x_cols(peer)], slot_at(outer, inner, 0, wide),
            w_send.at[step], w_recv.at[me], base + peer,
        ).start()

    def give_tail(step):
        peer = partner(inner, step, group)
        remote(
            tail_v.at[peer], slot_at(outer, inner, wide, main),
            w_send.at[step], w_recv.at[me], base + peer,
        ).start()

    def give_z(step):
        peer = partner(inner, step, group)
        for c in range(chunks):
            remote(
                w_own.at[:, z_cols(peer, c)], w_z.at[c, outer, at_rows(inner)],
                zg_send.at[step], zg_recv.at[inner], base + peer,
            ).start()

    load_all.wait()
    for step in range(1, group):
        give_x(step)
    load_bc.wait()

    @pl.when(has_up)
    def _():
        along(outer, 1).start()

    @pl.when(has_down)
    def _():
        along(outer, -1).start()

    tail_from = z_from + group * wide
    tail = w_own.shape[1] - tail_from
    row = lax.broadcasted_iota(jnp.int32, (tail, lanes), 0)
    col = lax.broadcasted_iota(jnp.int32, (tail, lanes), 1)
    narrow = w_own[:, tail_from:]
    for peer in range(group):
        steps_at = peer * hs + col
        levels_at = group * hs + peer * hs * levels + col - hs
        source = jnp.where(col < hs, steps_at, levels_at)
        source = jnp.where(col < hs + hs * levels, source, -1)
        pick = jnp.where(row == source, 1.0, 0.0).astype(bf16)
        tail_v[peer] = jnp.dot(narrow, pick, preferred_element_type=f32).astype(bf16)
    w_a[outer, at_rows(inner), wide:main] = tail_v[inner]
    load_x.wait()
    for step in range(1, group):
        give_tail(step)

    @pl.when(has_up)
    def _():
        up(outer, inner).start()

    @pl.when(has_down)
    def _():
        down(outer, inner).start()

    piece_rows = 32

    def norm(step, carry):
        at = pl.ds(pl.multiple_of(step * piece_rows, piece_rows), piece_rows)
        value = acts_ref[at].astype(f32)
        scale = lax.rsqrt(jnp.mean(value * value, axis=1, keepdims=True) + EPS)
        u_all[inner, at] = (value * scale * norm_ref[...]).astype(bf16)
        return carry

    lax.fori_loop(0, length // piece_rows, norm, 0)

    for step in range(1, group):
        slot = partner(inner, step, group)
        arrived(outer, slot)

        @pl.when(has_up)
        def _():
            up(outer, slot).start()

        @pl.when(has_down)
        def _():
            down(outer, slot).start()

    half_rows = length // 2

    def u_half(block, h):
        return u_all.at[block, h * half_rows : (h + 1) * half_rows]

    def u_copy(block, h, at, peer):
        piece = u_half(block, h)
        return remote(piece, piece, u_send.at[at], u_recv.at[block * 2 + h], base + peer)

    u_sends = [
        u_copy(inner, 1, 0, p1),
        u_copy(inner, 0, 1, p2),
        u_copy(inner, 0, 2, p1),
        u_copy(inner, 1, 3, p2),
    ]
    u_relays = [u_copy(p1, 1, 4, p2), u_copy(p2, 0, 5, p1)]

    def u_arrived(block, h):
        piece = u_half(block, h)
        remote(piece, piece, u_send.at[0], u_recv.at[block * 2 + h], me).wait_recv()

    for copy in u_sends:
        copy.start()
    for step in range(1, group):
        across(outer, step).start()

    for c in range(chunks):
        pltpu.make_async_copy(
            w_hbm.at[:, z_cols(inner, c)], w_z.at[c, outer, at_rows(inner)], load_sem.at[3]
        ).start()
    z_own = w_z.at[:, outer, at_rows(inner)]
    for c in range(chunks):
        for j in range(group):
            pltpu.make_async_copy(
                wo_hbm.at[j * wide + c * cw : j * wide + (c + 1) * cw],
                w_o.at[c, j * cw : (j + 1) * cw],
                load_sem.at[4],
            ).start()
    for step in range(1, group):
        give_z(step)
    picks[0] = selector(lanes, wide, size, 0, 1)

    def fill(level, carry):
        picks[level + 1] = selector(lanes, wide, size, hs + level, levels)
        return carry

    lax.fori_loop(0, used + 1, fill, 0)

    @pl.when(jnp.logical_not(has_down))
    def _():
        halo[...] = jnp.zeros(halo.shape, halo.dtype)

    def relay(distance, block):
        slot = partner(inner, block, group)

        @pl.when(outer - distance >= 0)
        def _():
            source = outer - distance
            arrived(source, slot)

            @pl.when(has_up)
            def _():
                up(source, slot).start()

            @pl.when(block == 0)
            def _():
                bc_arrived(source, inner)

                @pl.when(has_up)
                def _():
                    along(source, 1).start()

                for step in range(1, group):
                    across(source, step).start()

        @pl.when(outer + distance < outers)
        def _():
            source = outer + distance
            arrived(source, slot)

            @pl.when(has_down)
            def _():
                down(source, slot).start()

            @pl.when(block == 0)
            def _():
                bc_arrived(source, inner)

                @pl.when(has_down)
                def _():
                    along(source, -1).start()

                for step in range(1, group):
                    across(source, step).start()

    def relay_step(step, carry):
        relay(step // group, lax.rem(step, group))
        return carry

    def up_z(source, c):
        at = c * outers + source
        piece = w_z.at[c, source]
        return remote(piece, piece, zu_send.at[at], z_recv.at[at], me + group)

    def down_z(source, c):
        at = c * outers + source
        piece = w_z.at[c, source]
        return remote(piece, piece, zd_send.at[at], z_recv.at[at], me - group)

    def z_arrived(source, c):
        piece = w_z.at[c, source]
        remote(piece, piece, zu_send.at[0], z_recv.at[c * outers + source], me).wait_recv()

    def own_z(c):
        @pl.when(has_up)
        def _():
            up_z(outer, c).start()

        @pl.when(has_down)
        def _():
            down_z(outer, c).start()

    def service(c):
        def step_of(distance, carry):
            @pl.when(jnp.logical_and(outer - distance >= 0, has_up))
            def _():
                z_arrived(outer - distance, c)
                up_z(outer - distance, c).start()

            @pl.when(jnp.logical_and(outer + distance < outers, has_down))
            def _():
                z_arrived(outer + distance, c)
                down_z(outer + distance, c).start()

            return carry

        lax.fori_loop(1, outers - 1, step_of, 0)

    def settle(c):
        def step_of(distance, carry):
            @pl.when(jnp.logical_and(outer - distance >= 0, jnp.logical_not(has_up)))
            def _():
                z_arrived(outer - distance, c)

            @pl.when(jnp.logical_and(outer + distance < outers, jnp.logical_not(has_down)))
            def _():
                z_arrived(outer + distance, c)

            return carry

        lax.fori_loop(1, outers, step_of, 0)

    lax.fori_loop(group, min(2, outers) * group, relay_step, 0)
    u_arrived(p1, 1)
    u_relays[0].start()
    u_arrived(p2, 0)
    u_relays[1].start()
    if outers > 2:
        lax.fori_loop(2 * group, (outers - 1) * group, relay_step, 0)
    pltpu.make_async_copy(z_own, z_own, load_sem.at[3]).wait()
    for step in range(1, group):
        slot = partner(inner, step, group)
        piece = w_z.at[:, outer, at_rows(slot)]
        remote(piece, piece, zg_send.at[0], zg_recv.at[slot], me).wait_recv()
    own_z(0)
    own_z(1)
    if outers > 2:
        lax.fori_loop((outers - 1) * group, outers * group, relay_step, 0)
    own_z(2)
    service(0)
    u_arrived(p1, 0)
    u_arrived(p2, 1)

    def ready(source, carry):
        for step in range(1, group):
            bc_arrived(source, partner(inner, step, group))
        return carry

    lax.fori_loop(0, outers, ready, 0)

    def multiply(step, carry):
        block = partner(inner, step, group)
        every = w_a[...].reshape(outers * depth, columns)
        part = jnp.dot(u_all[block], every, preferred_element_type=f32)
        p_a[block] = part.astype(bf16)
        return carry

    lax.fori_loop(0, group - 1, multiply, 0)
    own_z(3)
    service(1)
    u_arrived(p3, 0)
    u_arrived(p3, 1)
    multiply(group - 1, 0)
    edge = remote(
        p_a.at[group - 1, length - keep :], halo, halo_sem.at[0], halo_sem.at[1], me + group
    )

    @pl.when(has_up)
    def _():
        edge.start()

    taps_x = taps_ref.at[:, x_cols(inner)]
    mine = jnp.concatenate([taps_x[...], taps_ref[:, bc_from:]], axis=1)
    mine_bias = jnp.concatenate(
        [cbias_ref[:, x_cols(inner)], cbias_ref[:, bc_from:]], axis=1
    )

    def state_work(step, carry):
        block = lax.rem(step + 1, group)

        @pl.when(jnp.logical_and(step == group - 1, has_down))
        def _():
            edge.wait_recv()

        @pl.when(block == 0)
        def _():
            before_s[...] = halo[...]

        @pl.when(block > 0)
        def _():
            before_s[...] = p_a[jnp.maximum(block - 1, 0), length - keep :]

        raw = jnp.concatenate([p_a[block, :, :wide], p_a[block, :, main:]], axis=1).astype(f32)
        last = before_s[...].astype(f32)
        last = jnp.concatenate([last[:, :wide], last[:, main:]], axis=1)
        ext = jnp.concatenate([last, raw], axis=0)
        first = keep - taps + 1
        mixed = mine_bias + mine[taps - 1 :] * raw
        for k in range(taps - 1):
            mixed = mixed + mine[k : k + 1] * ext[first + k : first + k + length]
        mixed = silu(mixed)
        x = mixed[:, :wide]
        x_s[block] = x.astype(bf16)
        bc = mixed[:, wide:].astype(bf16)
        bc_s[block] = bc
        small = softplus(p_a[block, :, wide:main].astype(f32) + small_bias_ref[inner])
        small_s[block] = small
        rows_at = lax.broadcasted_iota(jnp.int32, (length, length), 0)
        cols_at = lax.broadcasted_iota(jnp.int32, (length, length), 1)
        below = jnp.where(cols_at <= rows_at, 1.0, 0.0)
        cum = jnp.dot(
            below, -small * rate_ref[inner], precision=HIGHEST, preferred_element_type=f32
        )
        cum_s[block] = cum
        fade = jnp.exp(cum[length - 1 :] - cum) * small
        faded = (x * spread(fade, picks[0])).astype(bf16)
        st[block] = lax.dot_general(
            bc[:, :state], faded, (((0,), (0,)), ((), ())), preferred_element_type=f32
        )
        return carry

    lax.fori_loop(0, group, state_work, 0)
    service(2)

    def widened(log):
        value = jnp.broadcast_to(jnp.exp(log), (8, lanes))
        return jnp.dot(
            value, picks[0].astype(f32), precision=HIGHEST, preferred_element_type=f32
        )[:1]

    ends = [cum_s[b, length - 1 :] for b in range(group)]
    part_rows = 32
    logs = list(ends)
    before = [jnp.zeros_like(ends[0]) for _ in range(group)]
    plan = []
    for bit in range(bits):
        half = 1 << bit
        joins, uppers, next_logs = [], [], []
        for g in range(len(logs) // 2):
            for b in range(2 * g * half + half, 2 * (g + 1) * half):
                uppers.append((b, g, None if bit == 0 else widened(before[b])))
                before[b] = before[b] + logs[2 * g]
            joins.append(widened(logs[2 * g + 1]))
            next_logs.append(logs[2 * g] + logs[2 * g + 1])
        plan.append((joins, uppers))
        logs = next_logs
    block_log = logs[0]
    before_log = jnp.zeros_like(block_log)

    def local_join(step, carry):
        at = pl.ds(pl.multiple_of(step * part_rows, part_rows), part_rows)
        summed = [st[b, at] for b in range(group)]
        for bit, (joins, uppers) in enumerate(plan):
            taken = set()
            for b, g, factor in uppers:
                value = summed[2 * g]
                if factor is not None:
                    value = factor * value
                bucket[b, bit, at] = value.astype(bf16)
                taken.add(b)
            for b in range(group):
                if b not in taken:
                    bucket[b, bit, at] = jnp.zeros((part_rows, wide), bf16)
            summed = [
                factor * summed[2 * g] + summed[2 * g + 1] for g, factor in enumerate(joins)
            ]
        whole_st[at] = summed[0]
        if used > bits:
            xs_own[0, at] = summed[0].astype(bf16)
        return carry

    lax.fori_loop(0, state // part_rows, local_join, 0)

    def swap(k):
        peer = twin(bits + k)
        return (
            remote(xl_own.at[k], xl_got.at[k], xl_sem.at[2 * k], xl_sem.at[2 * k + 1], peer),
            remote(xs_own.at[k], xs_got.at[k], xs_sem.at[2 * k], xs_sem.at[2 * k + 1], peer),
        )

    def send_state(k):
        xl_own[k] = jnp.broadcast_to(block_log, (8, lanes))
        for copy in swap(k):
            copy.start()

    if used > bits:
        send_state(0)

    def inside(block, carry):
        bc = bc_s[block]
        scores = lax.dot_general(
            bc[:, state:], bc[:, :state], (((1,), (1,)), ((), ())), preferred_element_type=f32
        )
        rows_at = lax.broadcasted_iota(jnp.int32, (length, length), 0)
        cols_at = lax.broadcasted_iota(jnp.int32, (length, length), 1)
        causal = cols_at <= rows_at
        small = small_s[block]
        cum = cum_s[block]
        cum_rows = jnp.transpose(cum)
        x = x_s[block].astype(f32)
        stepped = (x * spread(small, picks[0])).astype(bf16)
        parts = []
        for h in range(hs):
            differ = cum[:, h : h + 1] - cum_rows[h : h + 1, :]
            weights = jnp.exp(jnp.where(causal, differ, -1e30)) * scores
            parts.append(
                jnp.dot(
                    weights.astype(bf16),
                    stepped[:, h * size : (h + 1) * size],
                    preferred_element_type=f32,
                )
            )
        y = jnp.concatenate(parts, axis=1)
        y_s[block] = y * spread(small, picks[1]) + skip_ref[inner] * x
        return carry

    lax.fori_loop(0, group, inside, 0)
    service(3)

    def reads(lo, hi):
        def work(block, carry):
            c = bc_s[block, :, state:]
            small = small_s[block]
            total = None
            for level in range(lo, hi):
                value = jnp.dot(c, bucket[block, level], preferred_element_type=f32)
                term = value * spread(small, picks[level + 2])
                total = term if total is None else total + term
            y_s[block] += total * spread(jnp.exp(cum_s[block]), picks[0])
            return carry

        lax.fori_loop(0, group, work, 0)

    done = 0
    for k in range(used - bits):
        if k > 0 and k == used - bits - 1:
            reads(done, bits + k)
            done = bits + k
        for copy in swap(k):
            copy.wait_recv()
        other_log = xl_got[k][:1]
        upper = lax.rem(me // (1 << (bits + k)), 2)
        is_upper = jnp.broadcast_to(upper, (1, wide)) == 1
        lane_upper = jnp.broadcast_to(upper, (1, lanes)) == 1
        factors = [
            jnp.where(is_upper, widened(before_log + before[b]), 0.0) for b in range(group)
        ]
        mine_by = jnp.where(is_upper, 1.0, widened(other_log))
        other_by = jnp.where(is_upper, widened(block_log), 1.0)
        more = k + 1 < used - bits

        def join(step, carry):
            at = pl.ds(pl.multiple_of(step * part_rows, part_rows), part_rows)
            other = xs_got[k, at].astype(f32)
            for b in range(group):
                bucket[b, bits + k, at] = (factors[b] * other).astype(bf16)
            if more:
                total = other_by * other + mine_by * whole_st[at]
                whole_st[at] = total
                xs_own[k + 1, at] = total.astype(bf16)
            return carry

        lax.fori_loop(0, state // part_rows, join, 0)
        before_log = jnp.where(lane_upper, before_log + other_log, before_log)
        block_log = block_log + other_log
        if more:
            send_state(k + 1)
    reads(done, used)

    def copy_to(c, step):
        peer = partner(inner, group - step, group)
        return remote(
            q_own.at[c, peer], q_got.at[c, inner],
            q_send.at[c * group + step], q_recv.at[c * group + inner], base + peer,
        )

    def gate(c, block):
        every = w_z[c].reshape(outers * depth, cw)
        z = jnp.dot(u_all[block], every, preferred_element_type=f32)
        z = z.astype(bf16).astype(f32)
        y = y_s[block, :, pl.ds(pl.multiple_of(c * cw, cw), cw)]
        return (y * silu(z)).astype(bf16)

    def gate_all(c):
        settle(c)

        def work(step, carry):
            block = partner(inner, group - step, group)
            q_own[c, block] = gate(c, block)

            @pl.when(step > 1)
            def _():
                copy_to(c, step - 1).start()

            return carry

        lax.fori_loop(1, group, work, 0)
        q_got[c, inner] = gate(c, inner)
        copy_to(c, group - 1).start()

    def collect(c):
        for step in range(1, group):
            peer = partner(inner, step, group)
            piece = q_got.at[c, peer]
            remote(
                piece, piece, q_send.at[0], q_recv.at[c * group + peer], me
            ).wait_recv()

    def joined(c, at):
        q = jnp.concatenate([q_got[c, j, at] for j in range(group)], axis=1).astype(f32)
        squares = jnp.sum(q * q, axis=1, keepdims=True)
        return (q * gate_ref[c]).astype(bf16), squares

    everything = pl.ds(0, length)
    gate_all(0)
    pltpu.make_async_copy(w_o, w_o, load_sem.at[4]).wait()
    o_acc[...] = jnp.zeros(o_acc.shape, f32)

    def rounds(c, squares):
        gate_all(c)
        collect(c - 1)
        q, more = joined(c - 1, everything)
        o_acc[...] += jnp.dot(q, w_o[c - 1], preferred_element_type=f32)
        return squares + more

    squares = lax.fori_loop(1, chunks, rounds, jnp.zeros((length, 1), f32))
    collect(chunks - 1)
    parts = 2
    part = length // parts
    following = lax.rem(section + 1, sections)
    handoffs = []
    for r in range(parts):
        at = pl.ds(r * part, part)
        q, more = joined(chunks - 1, at)
        total = o_acc[at] + jnp.dot(q, w_o[chunks - 1], preferred_element_type=f32)
        mean = (squares[r * part : (r + 1) * part] + more) / (wide * group)
        o_v[at] = (acts_ref[at].astype(f32) + total * lax.rsqrt(mean + EPS)).astype(bf16)
        copy = remote(
            o_v.at[at], out_ref.at[at], ho_send.at[r], ho_recv.at[r], following, "section"
        )
        handoffs.append(copy)
        if r > 0:
            handoffs[r - 1].start()
    handoffs[-1].start()

    def drain(at, carry):
        source = at // group
        slot = lax.rem(at, group)

        @pl.when(jnp.logical_and(has_up, source <= outer))
        def _():
            up(source, slot).wait_send()

            @pl.when(slot == 0)
            def _():
                along(source, 1).wait_send()

        @pl.when(jnp.logical_and(has_down, source >= outer))
        def _():
            down(source, slot).wait_send()

            @pl.when(slot == 0)
            def _():
                along(source, -1).wait_send()

        @pl.when(slot == 0)
        def _():
            for step in range(1, group):
                across(source, step).wait_send()

        return carry

    lax.fori_loop(0, n, drain, 0)

    def drain_z(at, carry):
        c = at // outers
        source = lax.rem(at, outers)

        @pl.when(jnp.logical_and(has_up, source <= outer))
        def _():
            up_z(source, c).wait_send()

        @pl.when(jnp.logical_and(has_down, source >= outer))
        def _():
            down_z(source, c).wait_send()

        return carry

    lax.fori_loop(0, chunks * outers, drain_z, 0)
    for step in range(1, group):
        piece = main_slot(outer, inner)
        remote(piece, piece, w_send.at[step], w_recv.at[me], me).wait_send()
        remote(z_own, z_own, zg_send.at[step], zg_recv.at[inner], me).wait_send()
        for c in range(chunks):
            copy_to(c, step).wait_send()
    for copy in u_sends + u_relays:
        copy.wait_send()

    @pl.when(has_up)
    def _():
        edge.wait_send()

    for k in range(used - bits):
        for copy in swap(k):
            copy.wait_send()
    for copy in handoffs:
        copy.wait()


def layer(dims, group, n, levels, used, sections, chunks, args):
    wide, state, size, taps, z_from, lanes = dims
    acts, w = args[0], args[1]
    length, width = acts.shape
    rows = w.shape[0]
    outers = n // group
    columns = wide + lanes + 2 * state
    cw = wide // chunks
    bits = group.bit_length() - 1
    swaps = max(used - bits, 1)
    dma = pltpu.SemaphoreType.DMA
    vmem = pl.BlockSpec(memory_space=pltpu.VMEM)
    anywhere = pl.BlockSpec(memory_space=pl.ANY)
    return pl.pallas_call(
        functools.partial(layer_kernel, dims, group, n, levels, used, sections),
        out_shape=jax.ShapeDtypeStruct((length, width), bf16),
        in_specs=[vmem, anywhere, anywhere] + [vmem] * (len(args) - 3),
        out_specs=vmem,
        scratch_shapes=[
            pltpu.VMEM((group, length, width), bf16),
            pltpu.VMEM(w.shape, bf16),
            pltpu.VMEM((group, rows, lanes), bf16),
            pltpu.VMEM((outers, group * rows, columns), bf16),
            pltpu.VMEM((chunks, outers, group * rows, cw), bf16),
            pltpu.VMEM((chunks, group * cw, width), bf16),
            pltpu.VMEM((group, length, columns), bf16),
            pltpu.VMEM((16, columns), bf16),
            pltpu.VMEM((16, columns), bf16),
            pltpu.VMEM((used + 2, lanes, wide), bf16),
            pltpu.VMEM((group, length, wide), bf16),
            pltpu.VMEM((group, length, 2 * state), bf16),
            pltpu.VMEM((group, length, lanes), f32),
            pltpu.VMEM((group, length, lanes), f32),
            pltpu.VMEM((group, state, wide), f32),
            pltpu.VMEM((group, used, state, wide), bf16),
            pltpu.VMEM((state, wide), f32),
            pltpu.VMEM((swaps, state, wide), bf16),
            pltpu.VMEM((swaps, state, wide), bf16),
            pltpu.VMEM((swaps, 8, lanes), f32),
            pltpu.VMEM((swaps, 8, lanes), f32),
            pltpu.VMEM((group, length, wide), f32),
            pltpu.VMEM((chunks, group, length, cw), bf16),
            pltpu.VMEM((chunks, group, length, cw), bf16),
            pltpu.VMEM((length, width), f32),
            pltpu.VMEM((length, width), bf16),
            dma((5,)),
            dma((6,)),
            dma((2 * group,)),
            dma((group,)),
            dma((n,)),
            dma((n,)),
            dma((n,)),
            dma((outers,)),
            dma((outers,)),
            dma((n,)),
            dma((n,)),
            dma((group,)),
            dma((group,)),
            dma((chunks * outers,)),
            dma((chunks * outers,)),
            dma((chunks * outers,)),
            dma((2,)),
            dma((2 * swaps,)),
            dma((2 * swaps,)),
            dma((chunks * group,)),
            dma((chunks * group,)),
            dma((2,)),
            dma((2,)),
        ],
        compiler_params=pltpu.CompilerParams(
            collective_id=0, has_side_effects=True, vmem_limit_bytes=60 << 20
        ),
    )(*args)


def per_device(
    acts,
    in_proj,
    out_proj,
    conv_weight,
    conv_bias,
    dt_bias,
    decay_rate,
    skip_gain,
    level_bias,
    norm_gain,
    gate_gain,
):
    n = lax.axis_size("seq")
    sections = lax.axis_size("section")
    group = min(4, n)
    inner = gate_gain.shape[1]
    heads = dt_bias.shape[1]
    head_size = inner // heads
    chans = conv_weight.shape[2]
    state = (chans - inner) // 2
    taps = conv_weight.shape[1]
    levels = level_bias.shape[1] // heads
    used = n.bit_length() - 1
    wide = inner // group
    hs = heads // group
    tail = hs + hs * levels
    lanes = -(-tail // 128) * 128
    chunks = wide // 128

    small_bias = jnp.concatenate(
        [dt_bias.reshape(group, 1, hs), level_bias.reshape(group, 1, hs * levels)], axis=2
    )
    small_bias = jnp.pad(small_bias, ((0, 0), (0, 0), (0, lanes - tail)))
    rate = jnp.pad(decay_rate.reshape(group, 1, hs), ((0, 0), (0, 0), (0, lanes - hs)))
    skip = jnp.repeat(skip_gain[0], head_size).reshape(group, 1, wide)
    gate = jnp.swapaxes(gate_gain.reshape(group, chunks, wide // chunks), 0, 1)
    gate = gate.reshape(chunks, 1, group * (wide // chunks))
    result = layer(
        (wide, state, head_size, taps, chans, lanes),
        group,
        n,
        levels,
        used,
        sections,
        chunks,
        (
            acts[0],
            in_proj[0],
            out_proj[0],
            conv_weight[0],
            conv_bias,
            small_bias,
            rate,
            skip,
            norm_gain,
            gate,
        ),
    )
    return result[None]


def solution(mesh):
    return jax.shard_map(
        per_device,
        mesh=mesh,
        in_specs=(
            P("section", "seq", None),
            P("section", "seq", None),
            P("section", None, None),
            P("section", None, None),
            P("section", None),
            P("section", None),
            P("section", None),
            P("section", None),
            P("section", None),
            P("section", None),
            P("section", None),
        ),
        out_specs=P("section", "seq", None),
        check_vma=False,
    )
```

time: 160 us -> 142 us (0.89)
  local copies, waits for them, and re-layouts: 19.1 us -> 8.2 us
  waiting for transfers between devices: 3.9 us -> 0 us
  other arithmetic: 9.32 us -> 5.96 us
  Pallas kernels: 124 us -> 127 us
  starting transfers between devices: 2.55 us -> 0 us
    unnamed x56 -> x3, local copies, waits for them, and re-layouts: 13.2 us -> 5.24 us
    another operation x7 -> x0, other arithmetic: 6.17 us -> none  [the longest x6 5.46 us: per_device(): stacked = jnp.stack([jnp.stack(held) for held in buckets]).astype(bf16)]
    unnamed x0 -> x4, other arithmetic: none -> 5.29 us
    ppermute x4 -> x0, waiting for transfers between devices: 3.9 us -> none  [the longest x1 2.65 us: passed_along(): return lax.ppermute(value, axis, pairs)]
    pallas_call x4 -> x1, Pallas kernels: 124 us -> 127 us  [layer(): pl.pallas_call(functools.partial(layer_kernel, dims, group, n, levels, us...]
    ppermute x4 -> x0, starting transfers between devices: 2.55 us -> none  [the longest x3 2.48 us: swapped(): return lax.ppermute(block, axis, route)]
    slice x11 -> x0, local copies, waits for them, and re-layouts: 2.52 us -> none  [the longest x1 0.78 us: per_device(): conv_weight[0][:, inner:]]
  transfers between devices with their start and end apart: 4 -> 0, of which waited for: 2 -> 0; matrix products, arithmetic and copies ran while one was open for 3% -> 0% of each run, Pallas kernels for 3% -> 0%
where the time goes in v1:
time: 142 us
  Pallas kernels  127 us (89%)
  local copies, waits for them, and re-layouts  8.2 us (6%)
  other arithmetic  5.96 us (4%)
    pallas_call x1, Pallas kernels, layer(): pl.pallas_call(functools.partial(layer_kernel, dims, group, n, levels, us...  127 us
    unnamed x4, other arithmetic  5.29 us
    unnamed x3, local copies, waits for them, and re-layouts  5.24 us

profile of v1, /device:TPU:0, one launch (start us, length us, event | category | flops | bytes accessed | tf_op | source)
XLA Modules:
  0.0 141.5 jit_solution(6734550388886193061)
XLA Ops:
  0.0 0.5 broadcast.26
  0.5 1.3 reduce.13
  1.8 1.3 reduce.14
  3.1 1.3 reduce.15
  4.5 1.3 reduce.12
  5.8 0.1 reshape.24
  5.9 0.1 broadcast_in_dim.10
  6.0 0.1 reshape.25
  6.1 0.6 pad.9.rate_ref
  6.7 0.1 reshape.23
  6.7 0.7 fusion.small_bias_ref
  7.4 1.3 copy.15
  8.7 0.1 broadcast_in_dim.11
  8.8 0.7 broadcast_in_dim.12.skip_ref
  9.4 2.4 %copy.12 = bf16[1,128,4640]{2,1,0:T(8,128)(2,1)} copy(bf16[1,128,4640]{1,2,0:T(8,128)(2,1)} %param.12) | data formatting | bytes 2375680 | tf_op args[1]
  11.9 127.4 %shard_map.109 = bf16[256,2048]{1,0:T(8,128)(2,1)} custom-call(bf16[256,2048]{1,0:T(8,128)(2,1)} %bitcast.14, bf16[128,4640]{1,0:T(8,128)(2,1)} %bitcast.12, bf16[2048,2048]{1,0:T(8,128)(2,1)} %bitcast.11, f32[4,2304]{1,0:T(4,128)} %bitcast.15, f32[1,2304]{1,0:T(1,128)} %cbias_ref.1, f32[4,1,128]{2,1,0:T(1,128)} %fusion.small_bias_ref, ...), custom_call_target="tpu_custom_call" | custom-call | tf_op jit(solution)/shard_map/pallas_call | solution.py:811
  139.2 2.3 %copy.17 = bf16[1,256,2048]{2,1,0:T(8,128)(2,1)} copy(bf16[1,256,2048]{2,1,0:T(8,128)(2,1)} %bitcast.13) | data formatting | bytes 2097152
